TPU v7x, 32 devices: a whole 2x2x4 slice. The times are simulated.
32 devices in a mesh: sec: 2 (over y), tp: 4 (over x, core), dp: 4 (over z).
Axes of the slice: x: 2, y: 2, z: 4, core: 2. Of those that a mesh axis runs over, the one named last changes fastest.
Arguments:
- feats: bfloat16 [8, 512, 512], P(('sec', 'dp'), 'tp'), may hold values from -6 to 6
- frame_clip: int32 [8, 32], P(('sec', 'dp')), may hold values from 0 to 3, never falling along the last dimension, each value on 1 to 16 neighbouring positions
- clip_order: int32 [8, 4], P(('sec', 'dp')), may hold values from 0 to 3, each once within a row
- conv_weight: bfloat16 [3, 512, 192], replicated, may hold values from -0.15625 to 0.15625
- embed_weight: bfloat16 [192, 3072], replicated, may hold values from -0.4375 to 0.4375
- wq: bfloat16 [3072, 512], P(('sec', 'dp'), 'tp')
- wk: bfloat16 [3072, 512], P(('sec', 'dp'), 'tp')
- wv: bfloat16 [3072, 512], P(('sec', 'dp'), 'tp'), may hold values from -0.109375 to 0.109375
- q_gain: float32 [4, 128], P('tp'), may hold values from 0.6 to 8, as said below
- k_gain: float32 [4, 128], P('tp'), may hold values from 0.6 to 8, as said below
Outputs:
- attended: bfloat16 [8, 512, 512], P(('sec', 'dp'), 'tp')
Inputs may be any that keep to these rules, and one draw needn't show every extreme that they name: `frame_clip`: clip ids never fall along the frames; every clip has at least one frame and one clip has exactly 16 frames. `clip_order`: each row holds every clip once. `q_gain`: positive. `k_gain`: positive.
All inputs are finite; a program needn't handle non-finite values.
Results may differ from a plain program's by a relative error of at most 0.0084.
Values may be sent and summed in bfloat16 or wider, within the bound.
A program may use at most 64 MiB of HBM per device.

v0:
```python
import jax
import jax.numpy as jnp
from jax import lax
from jax.sharding import PartitionSpec as P

HD = 128
PD = 192
TAPS = 3
VP = 16


def from_behind(value, axis, steps):
    count = lax.axis_size(axis)
    leading, last = (max(0, -steps), min(count, count - steps))
    return lax.ppermute(value, axis, [(source, source + steps) for source in range(leading, last)])


def packing(clip_ids, clip_order):
    frame_count = clip_ids.shape[0]
    clip_count = clip_order.shape[0]
    labels = jnp.arange(clip_count, dtype=jnp.int32)
    lengths = jnp.sum((clip_ids[None, :] == labels[:, None]).astype(jnp.int32), axis=1)
    starts = jnp.cumsum(lengths) - lengths
    picked = clip_order[:, None] == labels[None, :]
    packed_len = jnp.sum(jnp.where(picked, lengths[None, :], 0), axis=1)
    packed_from = jnp.sum(jnp.where(picked, starts[None, :], 0), axis=1)
    place_start = jnp.cumsum(packed_len) - packed_len
    frames = jnp.arange(frame_count, dtype=jnp.int32)
    places = jnp.sum((frames[:, None] >= place_start[None, :]).astype(jnp.int32), axis=1) - 1
    chosen = places[:, None] == labels[None, :]
    source = jnp.sum(jnp.where(chosen, (packed_from - place_start)[None, :], 0), axis=1) + frames
    return (source, places)


def normed(values, gains):
    scale = lax.rsqrt(jnp.mean(values * values, axis=-1, keepdims=True) + 1e-06)
    return (values * scale * gains[None, :]).astype(jnp.bfloat16)


def attend_local(projected, slots, segment, gain_q, gain_k):
    ordered = jnp.take(projected, slots, axis=0)
    query = normed(ordered[:, :HD], gain_q)
    key_rows = normed(ordered[:, HD : 2 * HD], gain_k)
    value_rows = ordered[:, 2 * HD :].astype(jnp.bfloat16)
    total = query.shape[0]
    block = min(total, 512)
    query_blocks = query.reshape(total // block, block, HD)
    segment_blocks = segment.reshape(total // block, block)

    def one_block(inputs):
        query_rows, block_seg = inputs
        scores = jnp.dot(query_rows, key_rows.T, preferred_element_type=jnp.float32) * HD ** (-0.5)
        same_seg = block_seg[:, None] == segment[None, :]
        scores = jnp.where(same_seg, scores, -1e30)
        highest = jnp.max(scores, axis=-1, keepdims=True)
        expo = jnp.where(same_seg, jnp.exp(scores - highest), 0.0)
        probs = (expo / jnp.sum(expo, axis=-1, keepdims=True)).astype(jnp.bfloat16)
        return jnp.dot(probs, value_rows, preferred_element_type=jnp.float32).astype(jnp.bfloat16)

    mixed = lax.map(one_block, (query_blocks, segment_blocks))
    return mixed.reshape(total, HD)


def embed_project(every_latent, embed_weight, w_qkv):
    all_tokens = jnp.dot(every_latent, embed_weight, preferred_element_type=jnp.float32).astype(
        jnp.bfloat16
    )
    return jnp.dot(all_tokens, w_qkv, preferred_element_type=jnp.float32)


def local(feats, frame_clip, clip_order, conv_weight, embed_weight, wq, wk, wv, q_gain, k_gain):
    feature = feats[0]
    row_count = feature.shape[0]
    frames_dev = row_count // VP
    reach = TAPS - 1
    rim_rows = from_behind(feature[row_count - reach * VP :], "tp", 1)
    widened = jnp.concatenate([rim_rows, feature], axis=0)
    clip_ids = frame_clip[0]
    padded = jnp.concatenate([jnp.full((reach,), -1, jnp.int32), clip_ids])
    window = lax.dynamic_slice_in_dim(padded, lax.axis_index("tp") * frames_dev, frames_dev + reach)
    own_ids = window[reach:]
    summed = jnp.zeros((row_count, PD), jnp.float32)
    for delay in range(TAPS):
        first = reach - delay
        earlier = widened[first * VP : (first + frames_dev) * VP]
        in_clip = jnp.repeat(window[first : first + frames_dev] == own_ids, VP)
        contrib = jnp.dot(earlier, conv_weight[delay], preferred_element_type=jnp.float32)
        summed = summed + jnp.where(in_clip[:, None], contrib, 0.0)
    latent = summed.astype(jnp.bfloat16)
    full_q, full_k, full_v = (
        lax.all_gather(wq, ("sec", "dp"), axis=0, tiled=True),
        lax.all_gather(wk, ("sec", "dp"), axis=0, tiled=True),
        lax.all_gather(wv, ("sec", "dp"), axis=0, tiled=True),
    )
    w_qkv = jnp.concatenate([full_q, full_k, full_v], axis=1)
    source, places = packing(clip_ids, clip_order[0])
    slots = (source[:, None] * VP + jnp.arange(VP, dtype=jnp.int32)[None, :]).reshape(-1)
    segment = jnp.repeat(places, VP)
    flat_latent = latent.reshape(row_count * PD // 128, 128)
    every_latent = lax.all_gather(flat_latent, "tp", axis=0, tiled=True).reshape(-1, PD)
    projected = embed_project(every_latent, embed_weight, w_qkv)
    mixed = attend_local(projected, slots, segment, q_gain[0], k_gain[0])
    regrouped = lax.all_to_all(mixed, "tp", split_axis=0, concat_axis=1, tiled=True)
    return regrouped[None]


def solution(mesh):
    return jax.shard_map(
        local,
        mesh=mesh,
        in_specs=(
            P(("sec", "dp"), "tp", None),
            P(("sec", "dp"), None),
            P(("sec", "dp"), None),
            P(),
            P(),
            P(("sec", "dp"), "tp"),
            P(("sec", "dp"), "tp"),
            P(("sec", "dp"), "tp"),
            P("tp", None),
            P("tp", None),
        ),
        out_specs=P(("sec", "dp"), "tp", None),
        check_vma=False,
    )
```

profile of v0, /device:TPU:0, one launch (start us, length us, event | category | flops | bytes accessed | tf_op | source)
XLA Modules:
  0.0 136.3 jit_solution(9821429094563022714)
XLA Ops:
  0.0 0.9 slice_bitcast_fusion
  0.9 2.4 %collective-permute-start = (bf16[32,512]{1,0:T(8,128)(2,1)S(1)}, bf16[32,512]{1,0:T(8,128)(2,1)S(1)}, u32[]{:S(2)}, u32[]{:S(2)}) collective-permute-start(bf16[32,512]{1,0:T(8,128)(2,1)S(1)} %slice_bitcast_fusion), channel_id=1, source_target_pairs={{0,4},{4,8},{8,12},{1,5},{5,9},{9,13},{2,6},{6,10},{10,14},{3,7},{... | collective-permute-start | bytes 98312 | tf_op jit(solution)/shard_map/ppermute | solution.py:15
  3.3 0.8 convert_reduce_fusion.1
  4.0 0.2 reduce-window.16
  4.2 0.9 select_reduce_fusion.1
  5.1 0.2 reduce-window.15
  5.7 34.9 %all_gather.15 = bf16[3072,128]{1,0:T(8,128)(2,1)S(1)} all-gather(bf16[384,128]{1,0:T(8,128)(2,1)} %param.17), channel_id=1, replica_groups=mesh['sec'=2,'tp'=4,'dp'=4] {'sec','dp'}, dimensions={0}, use_global_device_ids=true | all-gather | bytes 884736 | tf_op jit(solution)/shard_map/all_gather | solution.py:93
  40.6 34.3 %all_gather.14 = bf16[3072,128]{1,0:T(8,128)(2,1)S(1)} all-gather(bf16[384,128]{1,0:T(8,128)(2,1)} %param.16), channel_id=1, replica_groups=mesh['sec'=2,'tp'=4,'dp'=4] {'sec','dp'}, dimensions={0}, use_global_device_ids=true | all-gather | bytes 884736 | tf_op jit(solution)/shard_map/all_gather | solution.py:92
  75.0 35.1 %all_gather.13 = bf16[3072,128]{1,0:T(8,128)(2,1)} all-gather(bf16[384,128]{1,0:T(8,128)(2,1)S(1)} %copy-done.2), channel_id=1, replica_groups=mesh['sec'=2,'tp'=4,'dp'=4] {'sec','dp'}, dimensions={0}, use_global_device_ids=true | all-gather | bytes 884736 | tf_op jit(solution)/shard_map/all_gather | solution.py:91
  110.0 1.1 fusion.13
  111.9 1.1 fusion.8
  113.0 1.1 fusion.9
  114.4 5.6 %all_gather.12 = bf16[768,128]{1,0:T(8,128)(2,1)S(1)} all-gather(bf16[192,128]{1,0:T(8,128)(2,1)S(1)} %reshape.156), channel_id=1, replica_groups=mesh['sec'=2,'tp'=4,'dp'=4] {'tp'}, dimensions={0}, use_global_device_ids=true | all-gather | bytes 245760 | tf_op jit(solution)/shard_map/all_gather | solution.py:100
  120.0 0.9 reshape.157
  120.9 3.8 %fusion = f32[512,384]{1,0:T(8,128)S(1)} fusion(bf16[3072,128]{1,0:T(8,128)(2,1)S(1)} %all_gather.15, bf16[3072,128]{1,0:T(8,128)(2,1)S(1)} %all_gather.14, bf16[3072,128]{1,0:T(8,128)(2,1)} %all_gather.13, bf16[512,192]{1,0:T(8,128)(2,1)} %reshape.157, bf16[192,3072]{1,0:T(8,128)(2,1)S(1)} %copy-done), kind=kOutput, calls=%fused_computation.2 | convolution fusion | flops 1820590080 | bytes 4521984 | tf_op jit(solution)/shard_map/dot_general | solution.py:68
  124.7 1.6 %gather_fusion = f32[512,384]{1,0:T(8,128)S(1)} fusion(f32[512,384]{1,0:T(8,128)S(1)} %fusion, s32[1024]{0:T(1024)S(1)} %pad_clamp_fusion), kind=kCustom, calls=%fused_computation | custom fusion | bytes 1574912 | tf_op jit(solution)/shard_map/jit(_take)/gather | solution.py:41
  126.4 0.1 broadcast_select_fusion
  126.5 0.2 multiply_reduce_fusion.1
  126.7 0.3 copy-done.4
  127.0 0.4 fusion.31
  127.5 0.2 fusion.10
  127.7 0.5 convolution_convert_fusion.1
  128.2 7.3 %all_to_all.16 = bf16[4,128,128]{2,1,0:T(8,128)(2,1)S(1)} all-to-all(bf16[4,128,128]{2,1,0:T(8,128)(2,1)S(1)} %bitcast.33), channel_id=1, replica_groups=mesh['sec'=2,'tp'=4,'dp'=4] {'tp'}, dimensions={0} | all-to-all | bytes 262144 | tf_op jit(solution)/shard_map/all_to_all | solution.py:103
  135.6 0.7 broadcast_in_dim.128
  (36 shorter events, 1.5 us)
Async XLA Ops:
  0.0 120.9 %copy-start = (bf16[192,3072]{1,0:T(8,128)(2,1)S(1)}, bf16[192,3072]{1,0:T(8,128)(2,1)}, u32[]{:S(2)}) copy-start(bf16[192,3072]{1,0:T(8,128)(2,1)} %param.14) | copy-start | bytes 3538948
  0.0 75.0 %copy-start.2 = (bf16[384,128]{1,0:T(8,128)(2,1)S(1)}, bf16[384,128]{1,0:T(8,128)(2,1)}, u32[]{:S(2)}) copy-start(bf16[384,128]{1,0:T(8,128)(2,1)} %param.15) | copy-start | bytes 294916
  0.9 111.0 %collective-permute-start = (bf16[32,512]{1,0:T(8,128)(2,1)S(1)}, bf16[32,512]{1,0:T(8,128)(2,1)S(1)}, u32[]{:S(2)}, u32[]{:S(2)}) collective-permute-start(bf16[32,512]{1,0:T(8,128)(2,1)S(1)} %slice_bitcast_fusion), channel_id=1, source_target_pairs={{0,4},{4,8},{8,12},{1,5},{5,9},{9,13},{2,6},{6,10},{10,14},{3,7},{... | collective-permute-start | bytes 98312 | tf_op jit(solution)/shard_map/ppermute | solution.py:15
  5.7 104.3 %copy-start.1 = (bf16[1,128,512]{2,1,0:T(8,128)(2,1)S(1)}, bf16[1,128,512]{2,1,0:T(8,128)(2,1)}, u32[]{:S(2)}) copy-start(bf16[1,128,512]{2,1,0:T(8,128)(2,1)} %param.10) | copy-start | bytes 393220
  40.6 70.6 %copy-start.3 = (s32[1,32]{1,0:T(1,128)S(1)}, s32[1,32]{1,0:T(1,128)}, u32[]{:S(2)}) copy-start(s32[1,32]{1,0:T(1,128)} %param.11) | copy-start | bytes 388
  126.3 0.7 copy-start.4
  126.4 0.7 copy-start.5
where the time goes:
time: 137 us; the launch traced here: 136 us
  blocking collectives  117 us (85%)
  matrix products  8.16 us (6%)
  local copies, waits for them, and re-layouts  5.43 us (4%)
  other arithmetic  2.97 us (2%)
  starting transfers between devices  2.39 us (2%)
    all_gather x1, blocking collectives, local(): lax.all_gather(wq, ('sec', 'dp'), axis=0, tiled=True)  35.1 us
    all_gather x1, blocking collectives, local(): lax.all_gather(wv, ('sec', 'dp'), axis=0, tiled=True)  34.9 us
    all_gather x1, blocking collectives, local(): lax.all_gather(wk, ('sec', 'dp'), axis=0, tiled=True)  34.3 us
    all_to_all x1, blocking collectives, local(): lax.all_to_all(mixed, 'tp', split_axis=0, concat_axis=1, tiled=True)  7.29 us
    all_gather x1, blocking collectives, local(): lax.all_gather(flat_latent, 'tp', axis=0, tiled=True).reshape(-1, PD)  5.6 us
    dot_general x1, matrix products, embed_project(): return jnp.dot(all_tokens, w_qkv, preferred_element_type=jnp.float32)  3.81 us
    dot_general x3, matrix products, local(): jnp.dot(earlier, conv_weight[delay], preferred_element_type=jnp.float32)  3.42 us
  transfers between devices with their start and end apart: 1, of which 0 were waited for; matrix products, arithmetic and copies ran while one was open for 3% of the time, Pallas kernels for 0%

commit v1 on v0

--- a/solution.py
+++ b/solution.py
@@ -87,9 +87,34 @@
         contrib = jnp.dot(earlier, conv_weight[delay], preferred_element_type=jnp.float32)
         summed = summed + jnp.where(in_clip[:, None], contrib, 0.0)
     latent = summed.astype(jnp.bfloat16)
+
+    def review_the_screen(patch):
+        ready, wide_out, inter = (
+            lax.axis_size(("sec", "dp")),
+            lax.axis_index(("sec", "dp")),
+            patch.shape[0],
+        )
+        block_list = [(u, (u + 1) % ready) for u in range(ready)]
+        sides = [(u, (u - 1) % ready) for u in range(ready)]
+        row_out = jnp.zeros((*patch.shape[:0], ready * inter, *patch.shape[1:]), patch.dtype)
+        row_out = lax.dynamic_update_slice_in_dim(row_out, patch, wide_out * inter, axis=0)
+        after = met_up = patch
+        taken_in = ready // 2
+        for src_i in range(1, taken_in + 1):
+            after = lax.ppermute(after, axis_name=("sec", "dp"), perm=block_list)
+            row_out = lax.dynamic_update_slice_in_dim(
+                row_out, after, (wide_out - src_i) % ready * inter, axis=0
+            )
+            if src_i < ready - taken_in:
+                met_up = lax.ppermute(met_up, axis_name=("sec", "dp"), perm=sides)
+                row_out = lax.dynamic_update_slice_in_dim(
+                    row_out, met_up, (wide_out + src_i) % ready * inter, axis=0
+                )
+        return row_out
+
     full_q, full_k, full_v = (
         lax.all_gather(wq, ("sec", "dp"), axis=0, tiled=True),
-        lax.all_gather(wk, ("sec", "dp"), axis=0, tiled=True),
+        review_the_screen(wk),
         lax.all_gather(wv, ("sec", "dp"), axis=0, tiled=True),
     )
     w_qkv = jnp.concatenate([full_q, full_k, full_v], axis=1)

time: 137 us -> 132 us (0.964)
  blocking collectives: 117 us -> 81.3 us
  starting transfers between devices: 2.39 us -> 17 us
  waiting for transfers between devices: 0.01 us -> 9.79 us
  local copies, waits for them, and re-layouts: 5.43 us -> 12.1 us
    all_gather x1 -> x0, blocking collectives: 34.3 us -> none  [local(): lax.all_gather(wk, ('sec', 'dp'), axis=0, tiled=True)]
    ppermute x0 -> x7, starting transfers between devices: none -> 15.5 us  [the longest x3 12.5 us: review_the_screen(): met_up = lax.ppermute(met_up, axis_name=('sec', 'dp'), perm=sides)]
    ppermute x0 -> x7, waiting for transfers between devices: none -> 9.79 us  [the longest x4 9.78 us: review_the_screen(): after = lax.ppermute(after, axis_name=('sec', 'dp'), perm=block_list)]
    dynamic_update_slice x0 -> x8, local copies, waits for them, and re-layouts: none -> 5.11 us  [the longest x4 2.55 us: review_the_screen(): lax.dynamic_update_slice_in_dim(row_out, after, (wide_out - src_i) % read...]
    all_gather x1, blocking collectives: 34.9 us -> 33.2 us  [local(): lax.all_gather(wv, ('sec', 'dp'), axis=0, tiled=True)]
  transfers between devices with their start and end apart: 1 -> 8, of which waited for: 0 -> 3; matrix products, arithmetic and copies ran while one was open for 3% -> 11% of each run, Pallas kernels for 0% -> 0%
where the time goes in v1:
time: 132 us; the launch traced here: 131 us
  blocking collectives  81.3 us (62%)
  starting transfers between devices  17 us (13%)
  local copies, waits for them, and re-layouts  12.1 us (9%)
  waiting for transfers between devices  9.79 us (7%)
  matrix products  8.21 us (6%)
  other arithmetic  2.97 us (2%)
    all_gather x1, blocking collectives, local(): lax.all_gather(wq, ('sec', 'dp'), axis=0, tiled=True)  34.2 us
    all_gather x1, blocking collectives, local(): lax.all_gather(wv, ('sec', 'dp'), axis=0, tiled=True)  33.2 us
    ppermute x3, starting transfers between devices, review_the_screen(): met_up = lax.ppermute(met_up, axis_name=('sec', 'dp'), perm=sides)  12.5 us
    ppermute x4, waiting for transfers between devices, review_the_screen(): after = lax.ppermute(after, axis_name=('sec', 'dp'), perm=block_list)  9.78 us
    all_to_all x1, blocking collectives, local(): lax.all_to_all(mixed, 'tp', split_axis=0, concat_axis=1, tiled=True)  7.37 us
    all_gather x1, blocking collectives, local(): lax.all_gather(flat_latent, 'tp', axis=0, tiled=True).reshape(-1, PD)  6.46 us
    dot_general x1, matrix products, embed_project(): return jnp.dot(all_tokens, w_qkv, preferred_element_type=jnp.float32)  3.81 us
    dot_general x3, matrix products, local(): jnp.dot(earlier, conv_weight[delay], preferred_element_type=jnp.float32)  3.47 us
  transfers between devices with their start and end apart: 8, of which 3 were waited for; matrix products, arithmetic and copies ran while one was open for 11% of the time, Pallas kernels for 0%

profile of v1, /device:TPU:0, one launch (start us, length us, event | category | flops | bytes accessed | tf_op | source)
XLA Modules:
  0.0 131.5 jit_solution(10138315781990284085)
XLA Ops:
  0.0 3.1 %collective-permute-start.1 = (bf16[384,128]{1,0:T(8,128)(2,1)}, bf16[384,128]{1,0:T(8,128)(2,1)S(1)}, u32[]{:S(2)}, u32[]{:S(2)}) collective-permute-start(bf16[384,128]{1,0:T(8,128)(2,1)} %param.16), channel_id=1, source_target_pairs={{0,1},{1,2},{2,3},{3,16},{16,17},{17,18},{18,19},{19,0},{4,5},{5,6... | collective-permute-start | bytes 294920 | tf_op jit(solution)/shard_map/ppermute | solution.py:104
  3.1 3.0 %collective-permute-start.2 = (bf16[384,128]{1,0:T(8,128)(2,1)}, bf16[384,128]{1,0:T(8,128)(2,1)S(1)}, u32[]{:S(2)}, u32[]{:S(2)}) collective-permute-start(bf16[384,128]{1,0:T(8,128)(2,1)} %param.16), channel_id=1, source_target_pairs={{0,19},{1,0},{2,1},{3,2},{16,3},{17,16},{18,17},{19,18},{4,23},{5,... | collective-permute-start | bytes 294920 | tf_op jit(solution)/shard_map/ppermute | solution.py:109
  6.1 0.8 slice_bitcast_fusion
  6.9 1.4 %collective-permute-start = (bf16[32,512]{1,0:T(8,128)(2,1)S(1)}, bf16[32,512]{1,0:T(8,128)(2,1)S(1)}, u32[]{:S(2)}, u32[]{:S(2)}) collective-permute-start(bf16[32,512]{1,0:T(8,128)(2,1)S(1)} %slice_bitcast_fusion), channel_id=1, source_target_pairs={{0,4},{4,8},{8,12},{1,5},{5,9},{9,13},{2,6},{6,10},{10,14},{3,7},{... | collective-permute-start | bytes 98312 | tf_op jit(solution)/shard_map/ppermute | solution.py:15
  8.3 0.8 convert_reduce_fusion.1
  9.3 0.9 select_reduce_fusion.1
  10.8 0.7 pad_dynamic-slice_fusion
  11.6 1.2 fusion.13
  12.8 34.2 %all_gather.10 = bf16[3072,128]{1,0:T(8,128)(2,1)S(1)} all-gather(bf16[384,128]{1,0:T(8,128)(2,1)} %param.15), channel_id=1, replica_groups=mesh['sec'=2,'tp'=4,'dp'=4] {'sec','dp'}, dimensions={0}, use_global_device_ids=true | all-gather | bytes 884736 | tf_op jit(solution)/shard_map/all_gather | solution.py:116
  47.0 33.2 %all_gather.11 = bf16[3072,128]{1,0:T(8,128)(2,1)S(1)} all-gather(bf16[384,128]{1,0:T(8,128)(2,1)S(1)} %copy-done.2), channel_id=1, replica_groups=mesh['sec'=2,'tp'=4,'dp'=4] {'sec','dp'}, dimensions={0}, use_global_device_ids=true | all-gather | bytes 884736 | tf_op jit(solution)/shard_map/all_gather | solution.py:118
  80.3 1.0 broadcast_in_dim.128
  82.4 1.1 fusion.8
  83.5 1.1 fusion.9
  84.9 6.5 %all_gather.9 = bf16[768,128]{1,0:T(8,128)(2,1)S(1)} all-gather(bf16[192,128]{1,0:T(8,128)(2,1)S(1)} %reshape.156), channel_id=1, replica_groups=mesh['sec'=2,'tp'=4,'dp'=4] {'tp'}, dimensions={0}, use_global_device_ids=true | all-gather | bytes 245760 | tf_op jit(solution)/shard_map/all_gather | solution.py:125
  91.4 0.9 reshape.157
  92.3 4.7 %collective-permute-start.4 = (bf16[384,128]{1,0:T(8,128)(2,1)S(1)}, bf16[384,128]{1,0:T(8,128)(2,1)S(1)}, u32[]{:S(2)}, u32[]{:S(2)}) collective-permute-start(bf16[384,128]{1,0:T(8,128)(2,1)S(1)} %collective-permute-done.2), channel_id=1, source_target_pairs={{0,19},{1,0},{2,1},{3,2},{16,3},{17,16},{18,17},{19,18},{4,23},{5,... | collective-permute-start | bytes 294920 | tf_op jit(solution)/shard_map/ppermute | solution.py:109
  98.3 2.4 %collective-permute-done.3 = bf16[384,128]{1,0:T(8,128)(2,1)S(1)} collective-permute-done((bf16[384,128]{1,0:T(8,128)(2,1)S(1)}, bf16[384,128]{1,0:T(8,128)(2,1)S(1)}, u32[]{:S(2)}, u32[]{:S(2)}) %collective-permute-start.3) | collective-permute-done | bytes 98336 | tf_op jit(solution)/shard_map/ppermute | solution.py:104
  100.7 4.7 %collective-permute-start.6 = (bf16[384,128]{1,0:T(8,128)(2,1)S(1)}, bf16[384,128]{1,0:T(8,128)(2,1)S(1)}, u32[]{:S(2)}, u32[]{:S(2)}) collective-permute-start(bf16[384,128]{1,0:T(8,128)(2,1)S(1)} %collective-permute-done.4), channel_id=1, source_target_pairs={{0,19},{1,0},{2,1},{3,2},{16,3},{17,16},{18,17},{19,18},{4,23},{5,... | collective-permute-start | bytes 294920 | tf_op jit(solution)/shard_map/ppermute | solution.py:109
  106.7 1.4 %collective-permute-done.5 = bf16[384,128]{1,0:T(8,128)(2,1)S(1)} collective-permute-done((bf16[384,128]{1,0:T(8,128)(2,1)S(1)}, bf16[384,128]{1,0:T(8,128)(2,1)S(1)}, u32[]{:S(2)}, u32[]{:S(2)}) %collective-permute-start.5) | collective-permute-done | bytes 98336 | tf_op jit(solution)/shard_map/ppermute | solution.py:104
  109.4 6.0 %collective-permute-done.7 = bf16[384,128]{1,0:T(8,128)(2,1)S(1)} collective-permute-done((bf16[384,128]{1,0:T(8,128)(2,1)S(1)}, bf16[384,128]{1,0:T(8,128)(2,1)S(1)}, u32[]{:S(2)}, u32[]{:S(2)}) %collective-permute-start.7) | collective-permute-done | bytes 98336 | tf_op jit(solution)/shard_map/ppermute | solution.py:104
  116.0 3.8 %fusion = f32[512,384]{1,0:T(8,128)S(1)} fusion(bf16[3072,128]{1,0:T(8,128)(2,1)S(1)} %all_gather.11, bf16[3072,128]{1,0:T(8,128)(2,1)} %constant_dynamic-update-slice_fusion, bf16[3072,128]{1,0:T(8,128)(2,1)S(1)} %all_gather.10, bf16[512,192]{1,0:T(8,128)(2,1)} %reshape.157, bf16[192,3072]{1,0:T(8,128)(2,1)S(1)} %copy-done), kind=kOutput, calls=%fused_computation.2 | convolution fusion | flops 1820590080 | bytes 4521984 | tf_op jit(solution)/shard_map/dot_general | solution.py:68
  119.8 1.6 %gather_fusion = f32[512,384]{1,0:T(8,128)S(1)} fusion(f32[512,384]{1,0:T(8,128)S(1)} %fusion, s32[1024]{0:T(1024)S(1)} %pad_clamp_fusion), kind=kCustom, calls=%fused_computation | custom fusion | bytes 1574912 | tf_op jit(solution)/shard_map/jit(_take)/gather | solution.py:41
  123.3 7.4 %all_to_all.16 = bf16[4,128,128]{2,1,0:T(8,128)(2,1)S(1)} all-to-all(bf16[4,128,128]{2,1,0:T(8,128)(2,1)S(1)} %bitcast.33), channel_id=1, replica_groups=mesh['sec'=2,'tp'=4,'dp'=4] {'tp'}, dimensions={0} | all-to-all | bytes 262144 | tf_op jit(solution)/shard_map/all_to_all | solution.py:128
  130.8 0.7 broadcast_in_dim.132
  (58 shorter events, 8.7 us)
Async XLA Ops:
  0.0 116.0 %copy-start = (bf16[192,3072]{1,0:T(8,128)(2,1)S(1)}, bf16[192,3072]{1,0:T(8,128)(2,1)}, u32[]{:S(2)}) copy-start(bf16[192,3072]{1,0:T(8,128)(2,1)} %param.14) | copy-start | bytes 3538948
  0.0 47.0 %copy-start.2 = (bf16[384,128]{1,0:T(8,128)(2,1)S(1)}, bf16[384,128]{1,0:T(8,128)(2,1)}, u32[]{:S(2)}) copy-start(bf16[384,128]{1,0:T(8,128)(2,1)} %param.17) | copy-start | bytes 294916
  0.0 92.3 %collective-permute-start.1 = (bf16[384,128]{1,0:T(8,128)(2,1)}, bf16[384,128]{1,0:T(8,128)(2,1)S(1)}, u32[]{:S(2)}, u32[]{:S(2)}) collective-permute-start(bf16[384,128]{1,0:T(8,128)(2,1)} %param.16), channel_id=1, source_target_pairs={{0,1},{1,2},{2,3},{3,16},{16,17},{17,18},{18,19},{19,0},{4,5},{5,6... | collective-permute-start | bytes 294920 | tf_op jit(solution)/shard_map/ppermute | solution.py:104
  3.1 89.2 %collective-permute-start.2 = (bf16[384,128]{1,0:T(8,128)(2,1)}, bf16[384,128]{1,0:T(8,128)(2,1)S(1)}, u32[]{:S(2)}, u32[]{:S(2)}) collective-permute-start(bf16[384,128]{1,0:T(8,128)(2,1)} %param.16), channel_id=1, source_target_pairs={{0,19},{1,0},{2,1},{3,2},{16,3},{17,16},{18,17},{19,18},{4,23},{5,... | collective-permute-start | bytes 294920 | tf_op jit(solution)/shard_map/ppermute | solution.py:109
  6.9 75.5 %collective-permute-start = (bf16[32,512]{1,0:T(8,128)(2,1)S(1)}, bf16[32,512]{1,0:T(8,128)(2,1)S(1)}, u32[]{:S(2)}, u32[]{:S(2)}) collective-permute-start(bf16[32,512]{1,0:T(8,128)(2,1)S(1)} %slice_bitcast_fusion), channel_id=1, source_target_pairs={{0,4},{4,8},{8,12},{1,5},{5,9},{9,13},{2,6},{6,10},{10,14},{3,7},{... | collective-permute-start | bytes 98312 | tf_op jit(solution)/shard_map/ppermute | solution.py:15
  12.8 68.5 %copy-start.3 = (bf16[384,128]{1,0:T(8,128)(2,1)S(1)}, bf16[384,128]{1,0:T(8,128)(2,1)}, u32[]{:S(2)}) copy-start(bf16[384,128]{1,0:T(8,128)(2,1)} %param.16) | copy-start | bytes 294916
  47.0 35.4 %copy-start.1 = (bf16[1,128,512]{2,1,0:T(8,128)(2,1)S(1)}, bf16[1,128,512]{2,1,0:T(8,128)(2,1)}, u32[]{:S(2)}) copy-start(bf16[1,128,512]{2,1,0:T(8,128)(2,1)} %param.10) | copy-start | bytes 393220
  92.3 8.4 %collective-permute-start.3 = (bf16[384,128]{1,0:T(8,128)(2,1)S(1)}, bf16[384,128]{1,0:T(8,128)(2,1)S(1)}, u32[]{:S(2)}, u32[]{:S(2)}) collective-permute-start(bf16[384,128]{1,0:T(8,128)(2,1)S(1)} %collective-permute-done.1), channel_id=1, source_target_pairs={{0,1},{1,2},{2,3},{3,16},{16,17},{17,18},{18,19},{19,0},{4,5},{5,6... | collective-permute-start | bytes 294920 | tf_op jit(solution)/shard_map/ppermute | solution.py:104
  92.3 8.4 %collective-permute-start.4 = (bf16[384,128]{1,0:T(8,128)(2,1)S(1)}, bf16[384,128]{1,0:T(8,128)(2,1)S(1)}, u32[]{:S(2)}, u32[]{:S(2)}) collective-permute-start(bf16[384,128]{1,0:T(8,128)(2,1)S(1)} %collective-permute-done.2), channel_id=1, source_target_pairs={{0,19},{1,0},{2,1},{3,2},{16,3},{17,16},{18,17},{19,18},{4,23},{5,... | collective-permute-start | bytes 294920 | tf_op jit(solution)/shard_map/ppermute | solution.py:109
  100.7 7.4 %collective-permute-start.5 = (bf16[384,128]{1,0:T(8,128)(2,1)S(1)}, bf16[384,128]{1,0:T(8,128)(2,1)S(1)}, u32[]{:S(2)}, u32[]{:S(2)}) collective-permute-start(bf16[384,128]{1,0:T(8,128)(2,1)S(1)} %collective-permute-done.3), channel_id=1, source_target_pairs={{0,1},{1,2},{2,3},{3,16},{16,17},{17,18},{18,19},{19,0},{4,5},{5,6... | collective-permute-start | bytes 294920 | tf_op jit(solution)/shard_map/ppermute | solution.py:104
  100.7 8.0 %collective-permute-start.6 = (bf16[384,128]{1,0:T(8,128)(2,1)S(1)}, bf16[384,128]{1,0:T(8,128)(2,1)S(1)}, u32[]{:S(2)}, u32[]{:S(2)}) collective-permute-start(bf16[384,128]{1,0:T(8,128)(2,1)S(1)} %collective-permute-done.4), channel_id=1, source_target_pairs={{0,19},{1,0},{2,1},{3,2},{16,3},{17,16},{18,17},{19,18},{4,23},{5,... | collective-permute-start | bytes 294920 | tf_op jit(solution)/shard_map/ppermute | solution.py:109
  108.1 7.3 %collective-permute-start.7 = (bf16[384,128]{1,0:T(8,128)(2,1)S(1)}, bf16[384,128]{1,0:T(8,128)(2,1)S(1)}, u32[]{:S(2)}, u32[]{:S(2)}) collective-permute-start(bf16[384,128]{1,0:T(8,128)(2,1)S(1)} %collective-permute-done.5), channel_id=1, source_target_pairs={{0,1},{1,2},{2,3},{3,16},{16,17},{17,18},{18,19},{19,0},{4,5},{5,6... | collective-permute-start | bytes 294920 | tf_op jit(solution)/shard_map/ppermute | solution.py:104
  121.4 0.7 copy-start.4
  121.5 0.7 copy-start.5
